TPU v7x, 32 devices: a whole 2x2x4 slice. The times are simulated.
32 devices in a mesh: ctx: 8 (over z, x), kv: 2 (over y), pb: 2 (over core).
Axes of the slice: x: 2, y: 2, z: 4, core: 2. Of those that a mesh axis runs over, the one named last changes fastest.
Arguments:
- queries: bfloat16 [2, 8, 256, 128], P('kv', None, 'pb'), may hold values from -24 to 24
- cache_keys: bfloat16 [2, 32768, 128], P('kv', 'ctx'), may hold values from -6 to 6
- cache_values: bfloat16 [2, 32768, 128], P('kv', 'ctx'), may hold values from -6 to 6
- sel_index: int32 [2, 512], P('kv', 'ctx'), may hold values from 0 to 32767, as said below
Outputs:
- gram: float32 [2, 512, 512], P('kv', ('ctx', 'pb'))
- value_rhs: float32 [2, 512, 128], P('kv', ('ctx', 'pb'))
- mass_gap: float32 [2, 8, 256], P('kv', None, 'pb')
Inputs may be any that keep to these rules, and one draw needn't show every extreme that they name: `sel_index`: for every KV head, entries k * 64 to (k + 1) * 64 - 1 are distinct positions of context block k (from k * 4096 to (k + 1) * 4096 - 1), in increasing order.
All inputs are finite; a program needn't handle non-finite values.
Results may differ from a plain program's by a relative error of at most 0.0016.
Values may be sent and summed in bfloat16 or wider, within the bound.
A program may use at most 64 MiB of HBM per device.

v0:
```python
import functools
import math

import jax
import jax.numpy as jnp
from jax import lax
from jax.experimental import pallas as pl
from jax.experimental.pallas import tpu as pltpu
from jax.sharding import PartitionSpec as P

MESH = pl.DeviceIdType.MESH
eps = 1e-06
f32 = jnp.float32
bf16 = jnp.bfloat16


def dot_nt(a, b):
    return lax.dot_general(a, b, (((1,), (1,)), ((), ())), preferred_element_type=f32)


def fold(x, op):
    rows, cols = x.shape
    return op(x.reshape(rows // 8, 8, cols), axis=0)


def kernel(
    cfg, q_hbm, k_hbm, v_hbm, sel_hbm, gram_ref, rhs_ref, gap_ref,
    q_ref, k_ref, v_ref, sel_ref, vt, scores, comp, both, xrecv, zsend, zrecv, feat, gpart, grecv,
    rpart, precv, rsend, rrecv, in_sem,
    csend_sem, crecv_sem, xsend_sem, xrecv_sem, zsend_sem, zrecv_sem, gsend_sem, grecv_sem,
    psend_sem, precv_sem, rsend_sem, rrecv_sem,
):
    loads = [
        pltpu.make_async_copy(src, dst, in_sem.at[i])
        for i, (src, dst) in enumerate(
            ((sel_hbm, sel_ref), (k_hbm, k_ref), (q_hbm, q_ref), (v_hbm, v_ref))
        )
    ]
    for load in loads:
        load.start()
    n, npb = cfg["n"], cfg["npb"]
    rows, width = q_ref.shape
    keys = k_ref.shape[0]
    sel_dev = sel_ref.shape[1]
    sel_all = n * sel_dev
    piece = sel_dev // npb
    chunk = rows // n
    per = cfg["per"]
    block = per * chunk
    groups = n // per
    scale = width ** (-0.5)
    c2 = scale * math.log2(math.e)
    tile = cfg["tile"]
    inverse = 1.0 / (rows * npb)

    me = lax.axis_index("ctx")
    pb = lax.axis_index("pb")
    my_group = me // per
    my_pair = me // 2
    side = lax.rem(me, 2)

    barrier = pltpu.get_barrier_semaphore()

    def greet(j, carry):
        for d in range(npb):
            @pl.when(jnp.logical_or(j > 0, d > 0))
            def _():
                pl.semaphore_signal(
                    barrier, inc=1,
                    device_id={"ctx": lax.rem(me + j, n), "pb": lax.rem(pb + d, npb)},
                    device_id_type=MESH,
                )
        return carry

    lax.fori_loop(0, n, greet, 0)

    loads[0].wait()
    loads[1].wait()
    pos = (sel_ref[...] - me * keys).astype(f32)
    diag = lax.broadcasted_iota(jnp.int32, (sel_dev, sel_dev), 0) == lax.broadcasted_iota(
        jnp.int32, (sel_dev, sel_dev), 1
    )
    column = jnp.sum(jnp.where(diag, pos, 0.0), axis=1, keepdims=True).astype(jnp.int32)
    picked = jnp.zeros((sel_dev, width), f32)
    for t in range(0, keys, tile):
        hot = (lax.broadcasted_iota(jnp.int32, (sel_dev, tile), 1) + t == column).astype(f32).astype(bf16)
        picked += jnp.dot(hot, k_ref[t : t + tile, :], preferred_element_type=f32)
    comp[me] = picked.astype(bf16)
    loads[3].wait()
    for t in range(0, keys, tile):
        vt[:, t : t + tile] = v_ref[t : t + tile, :].T

    pl.semaphore_wait(barrier, n * npb - 1)

    def comp_copy(j, src):
        return pltpu.make_async_remote_copy(
            src_ref=comp.at[src], dst_ref=comp.at[src],
            send_sem=csend_sem.at[j], recv_sem=crecv_sem.at[src],
            device_id={"ctx": j}, device_id_type=MESH,
        )

    def x_copy(a):
        return pltpu.make_async_remote_copy(
            src_ref=both.at[a, 1 - side], dst_ref=xrecv.at[a],
            send_sem=xsend_sem.at[a], recv_sem=xrecv_sem.at[a],
            device_id={"ctx": me + 1 - 2 * side}, device_id_type=MESH,
        )

    def z_copy(a, src):
        return pltpu.make_async_remote_copy(
            src_ref=zsend.at[a], dst_ref=zrecv.at[src],
            send_sem=zsend_sem.at[a], recv_sem=zrecv_sem.at[src],
            device_id={"ctx": 2 * a + side}, device_id_type=MESH,
        )

    def merge(parts):
        top = parts[0][width : width + 1, :]
        for part in parts[1:]:
            top = jnp.maximum(top, part[width : width + 1, :])
        total, summed = 0.0, 0.0
        for part in parts:
            weight = jnp.exp2((part[width : width + 1, :] - top) * c2)
            total += weight * part[width + 1 : width + 2, :]
            summed += weight * part[:width, :]
        return top, total, summed

    def put(ref, index, top, total, summed):
        ref[index + (slice(0, width),)] = summed
        ref[index + (slice(width, width + 8),)] = jnp.concatenate(
            [top, total, jnp.zeros((6, chunk), f32)], axis=0
        )

    def pass_on(t):
        first = group_of(t) * (per // 2)
        for u in range(per // 2):
            a = first + u
            x_copy(a).wait_recv()
            merged = merge([both[a, side], xrecv[a]])
            if t == groups - 1:
                @pl.when(a == my_pair)
                def _():
                    put(zrecv, (my_pair,), *merged)

                @pl.when(a != my_pair)
                def _():
                    put(zsend, (a,), *merged)
                    z_copy(a, my_pair).start()
            else:
                put(zsend, (a,), *merged)
                z_copy(a, my_pair).start()

    def send_comp(d, carry):
        comp_copy(lax.rem(me + d, n), me).start()
        return carry

    lax.fori_loop(1, n, send_comp, 0)

    def group_of(t):
        return lax.rem(my_group + 1 + t, groups)

    def load_q(t):
        return q_ref[pl.ds(pl.multiple_of(group_of(t) * block, block), block), :]

    def score_tile(t, q, i, top):
        s = dot_nt(k_ref[i : i + tile, :], q)
        scores[t % 2, i : i + tile, :] = s
        part = fold(s, jnp.max)
        return part if top is None else jnp.maximum(top, part)

    loads[2].wait()
    q = load_q(0)
    top = None
    for i in range(0, keys, tile):
        top = score_tile(0, q, i, top)
    for t in range(groups):
        row_max = jnp.max(top, axis=0, keepdims=True)
        shift = row_max * c2
        total = jnp.zeros((8, block), f32)
        acc = jnp.zeros((width, block), f32)
        top = None
        if t + 1 < groups:
            q = load_q(t + 1)
        for i in range(0, keys, tile):
            p = jnp.exp2(scores[t % 2, i : i + tile, :] * c2 - shift)
            total += fold(p, jnp.sum)
            acc += jnp.dot(vt[:, i : i + tile], p.astype(bf16), preferred_element_type=f32)
            if t + 1 < groups:
                top = score_tile(t + 1, q, i, top)
        row_total = jnp.sum(total, axis=0, keepdims=True)
        first = group_of(t) * (per // 2)
        for u in range(per // 2):
            for e in range(2):
                lanes = slice((2 * u + e) * chunk, (2 * u + e + 1) * chunk)
                put(both, (first + u, e), row_max[:, lanes], row_total[:, lanes], acc[:, lanes])
            x_copy(first + u).start()
        if t > 0:
            pass_on(t - 1)

    def wait_comp(d, carry):
        src = lax.rem(me + d, n)
        comp_copy(src, src).wait_recv()
        return carry

    lax.fori_loop(1, n, wait_comp, 0)
    compact = comp[...].reshape(sel_all, width)

    def features(q):
        c = dot_nt(compact, q)
        cmax = jnp.max(c, axis=0, keepdims=True)
        e = jnp.exp2(c * c2 - cmax * c2)
        ctotal = jnp.sum(e, axis=0, keepdims=True)
        return (e * (sel_all / ctotal)).astype(bf16), cmax * scale + jnp.log(ctotal)

    gram = jnp.zeros((sel_dev, sel_all), f32)
    for g in range(groups):
        feat[g] = features(q_ref[g * block : (g + 1) * block, :])[0]
    for g in range(groups):
        own = feat[g, pl.ds(pl.multiple_of(me * sel_dev, sel_dev), sel_dev), :]
        gram += dot_nt(own, feat[g])
    for d in range(npb):
        gpart[d] = gram[d * piece : (d + 1) * piece, :] * inverse

    def g_copy(d, src):
        return pltpu.make_async_remote_copy(
            src_ref=gpart.at[d], dst_ref=grecv.at[src],
            send_sem=gsend_sem.at[d], recv_sem=grecv_sem.at[src],
            device_id={"pb": d}, device_id_type=MESH,
        )

    for d in range(1, npb):
        g_copy(lax.rem(pb + d, npb), pb).start()

    own_feat, own_mass = features(q_ref[pl.ds(pl.multiple_of(me * chunk, chunk), chunk), :])

    pass_on(groups - 1)

    def wait_z(d, carry):
        src = lax.rem(my_pair + d, n // 2)
        z_copy(src, src).wait_recv()
        return carry

    lax.fori_loop(1, n // 2, wait_z, 0)
    top, total, summed = merge([zrecv[b] for b in range(n // 2)])
    target = summed / total
    y = (target * lax.rsqrt(jnp.mean(target * target, axis=0, keepdims=True) + eps)).astype(bf16)
    gap = top * scale + jnp.log(total) - own_mass
    gap8 = jnp.broadcast_to(gap, (8, chunk))
    rhs = dot_nt(own_feat, y) * inverse

    def p_copy(d, src):
        return pltpu.make_async_remote_copy(
            src_ref=rpart.at[d], dst_ref=precv.at[src],
            send_sem=psend_sem.at[d], recv_sem=precv_sem.at[src],
            device_id={"pb": d}, device_id_type=MESH,
        )

    for d in range(npb):
        for j in range(n):
            start = (j * npb + d) * piece
            rpart[d, j] = rhs[start : start + piece, :]
    for d in range(1, npb):
        p_copy(lax.rem(pb + d, npb), pb).start()

    def r_copy(j, src):
        return pltpu.make_async_remote_copy(
            src_ref=rsend.at[j], dst_ref=rrecv.at[src],
            send_sem=rsend_sem.at[j], recv_sem=rrecv_sem.at[src],
            device_id={"ctx": j}, device_id_type=MESH,
        )

    for d in range(1, npb):
        p_copy(pb, lax.rem(pb + d, npb)).wait_recv()
    for j in range(n):
        part = rpart[pb, j]
        for d in range(1, npb):
            part += precv[lax.rem(pb + d, npb), j]
        rsend[j, :piece, :] = part
        rsend[j, piece:, :chunk] = gap8

    def send_r(d, carry):
        r_copy(lax.rem(me + d, n), me).start()
        return carry

    lax.fori_loop(1, n, send_r, 0)
    rrecv[me] = rsend[me]

    for d in range(1, npb):
        g_copy(pb, lax.rem(pb + d, npb)).wait_recv()
    result = gpart[pb]
    for d in range(1, npb):
        result += grecv[lax.rem(pb + d, npb)]
    gram_ref[...] = result
    for d in range(1, npb):
        g_copy(lax.rem(pb + d, npb), pb).wait_send()

    for d in range(1, npb):
        p_copy(lax.rem(pb + d, npb), pb).wait_send()

    def drain(d, carry):
        comp_copy(lax.rem(me + d, n), me).wait_send()
        return carry

    lax.fori_loop(1, n, drain, 0)

    def drain_x(a, carry):
        x_copy(a).wait_send()
        return carry

    lax.fori_loop(0, n // 2, drain_x, 0)

    def drain_z(d, carry):
        z_copy(lax.rem(my_pair + d, n // 2), my_pair).wait_send()
        return carry

    lax.fori_loop(1, n // 2, drain_z, 0)

    def wait_r(d, carry):
        src = lax.rem(me + d, n)
        r_copy(src, src).wait_recv()
        return carry

    lax.fori_loop(1, n, wait_r, 0)
    out = jnp.zeros((piece, width), f32)
    for j in range(n):
        out += rrecv[j, :piece, :]
        gap_ref[j : j + 1, :] = rrecv[j, piece : piece + 1, :chunk]
    rhs_ref[...] = out

    def drain_r(d, carry):
        r_copy(lax.rem(me + d, n), me).wait_send()
        return carry

    lax.fori_loop(1, n, drain_r, 0)


def solution(mesh):
    n, npb = mesh.shape["ctx"], mesh.shape["pb"]

    def shards(queries, cache_keys, cache_values, sel_index):
        heads, rows_dev, width = queries.shape[1:]
        rows = heads * rows_dev
        keys = cache_keys.shape[1]
        sel_dev = sel_index.shape[1]
        sel_all, piece, chunk = sel_dev * n, sel_dev // npb, rows // n
        per = max(2, min(n, 256 // chunk))
        while n % per or per % 2:
            per -= 1
        block = per * chunk
        tile = math.gcd(keys, 512)
        cfg = dict(n=n, npb=npb, per=per, tile=tile)
        vmem = pl.BlockSpec(memory_space=pltpu.VMEM)
        dma = pltpu.SemaphoreType.DMA
        gram, rhs, gap = pl.pallas_call(
            functools.partial(kernel, cfg),
            out_shape=(
                jax.ShapeDtypeStruct((piece, sel_all), f32),
                jax.ShapeDtypeStruct((piece, width), f32),
                jax.ShapeDtypeStruct((n, chunk), f32),
            ),
            in_specs=[pl.BlockSpec(memory_space=pltpu.HBM)] * 4,
            out_specs=(vmem,) * 3,
            scratch_shapes=[
                pltpu.VMEM((rows, width), bf16),
                pltpu.VMEM((keys, width), bf16),
                pltpu.VMEM((keys, width), bf16),
                pltpu.VMEM((1, sel_dev), jnp.int32),
                pltpu.VMEM((width, keys), bf16),
                pltpu.VMEM((2, keys, block), f32),
                pltpu.VMEM((n, sel_dev, width), bf16),
                pltpu.VMEM((n // 2, 2, width + 8, chunk), f32),
                pltpu.VMEM((n // 2, width + 8, chunk), f32),
                pltpu.VMEM((n // 2, width + 8, chunk), f32),
                pltpu.VMEM((n // 2, width + 8, chunk), f32),
                pltpu.VMEM((n // per, sel_all, block), bf16),
                pltpu.VMEM((npb, piece, sel_all), f32),
                pltpu.VMEM((npb, piece, sel_all), f32),
                pltpu.VMEM((npb, n, piece, width), f32),
                pltpu.VMEM((npb, n, piece, width), f32),
                pltpu.VMEM((n, piece + 8, width), f32),
                pltpu.VMEM((n, piece + 8, width), f32),
                dma((4,)),
                dma((n,)), dma((n,)), dma((n // 2,)), dma((n // 2,)), dma((n // 2,)), dma((n // 2,)),
                dma((npb,)), dma((npb,)), dma((npb,)), dma((npb,)), dma((n,)), dma((n,)),
            ],
            compiler_params=pltpu.CompilerParams(
                collective_id=0, has_side_effects=True, vmem_limit_bytes=50 * 1024 * 1024
            ),
        )(queries[0].reshape(rows, width), cache_keys[0], cache_values[0], sel_index)
        return gram[None], rhs[None], gap.reshape(1, heads, rows_dev)

    in_specs = (
        P("kv", None, "pb", None),
        P("kv", "ctx", None),
        P("kv", "ctx", None),
        P("kv", "ctx"),
    )
    out_specs = (P("kv", ("ctx", "pb"), None), P("kv", ("ctx", "pb"), None), P("kv", None, "pb"))
    return jax.shard_map(shards, mesh=mesh, in_specs=in_specs, out_specs=out_specs, check_vma=False)
```

profile of v0, /device:TPU:1, one launch (start us, length us, event | category | flops | bytes accessed | tf_op | source)
XLA Modules:
  0.0 33.7 jit_solution(7680276960591890525)
XLA Ops:
  0.6 0.0 copy-start.3
  0.6 0.6 %copy-done.3 = s32[1,64]{1,0:T(1,128)S(1)} copy-done((s32[1,64]{1,0:T(1,128)S(1)}, s32[1,64]{1,0:T(1,128)}, u32[]{:S(2)}) %copy-start.3) | copy-done | bytes 280
  1.3 0.0 copy-start
  1.3 1.2 %copy-done = bf16[1,4096,128]{2,1,0:T(8,128)(2,1)S(1)} copy-done((bf16[1,4096,128]{2,1,0:T(8,128)(2,1)S(1)}, bf16[1,4096,128]{2,1,0:T(8,128)(2,1)}, u32[]{:S(2)}) %copy-start) | copy-done | bytes 1048600
  2.5 0.0 copy-start.1
  2.5 1.2 %copy-done.1 = bf16[1,4096,128]{2,1,0:T(8,128)(2,1)S(1)} copy-done((bf16[1,4096,128]{2,1,0:T(8,128)(2,1)S(1)}, bf16[1,4096,128]{2,1,0:T(8,128)(2,1)}, u32[]{:S(2)}) %copy-start.1) | copy-done | bytes 1048600
  3.7 0.0 copy-start.2
  3.7 0.9 %copy-done.2 = bf16[1,8,128,128]{3,2,1,0:T(8,128)(2,1)S(1)} copy-done((bf16[1,8,128,128]{3,2,1,0:T(8,128)(2,1)S(1)}, bf16[1,8,128,128]{3,2,1,0:T(8,128)(2,1)}, u32[]{:S(2)}) %copy-start.2) | copy-done | bytes 262168
  4.7 27.2 %shard_map.67 = (f32[32,512]{1,0:T(8,128)S(1)}, f32[32,128]{1,0:T(8,128)S(1)}, f32[8,128]{1,0:T(8,128)S(1)}) custom-call(bf16[1024,128]{1,0:T(8,128)(2,1)S(1)} %bitcast.8, bf16[4096,128]{1,0:T(8,128)(2,1)S(1)} %bitcast.6, bf16[4096,128]{1,0:T(8,128)(2,1)S(1)} %bitcast.7, s32[1,64]{1,0:T(1,128)S(1)} %copy-done.3), custom_call_target="tpu_custom_call" | custom-call | tf_op jit(solution)/shard_map/pallas_call | solution.py:353
  31.9 0.6 %copy.10 = f32[1,32,512]{2,1,0:T(8,128)} copy(f32[1,32,512]{2,1,0:T(8,128)S(1)} %bitcast.9) | data formatting | bytes 131072
  32.5 0.6 %copy.11 = f32[1,32,128]{2,1,0:T(8,128)} copy(f32[1,32,128]{2,1,0:T(8,128)S(1)} %bitcast.10) | data formatting | bytes 32768
  33.1 0.6 %copy.12 = f32[1,8,128]{2,1,0:T(8,128)} copy(f32[1,8,128]{2,1,0:T(8,128)S(1)} %bitcast.11) | data formatting | bytes 8192
Async XLA Ops:
  0.6 0.7 %copy-start.3 = (s32[1,64]{1,0:T(1,128)S(1)}, s32[1,64]{1,0:T(1,128)}, u32[]{:S(2)}) copy-start(s32[1,64]{1,0:T(1,128)} %sel_hbm.1) | copy-start | bytes 772
  1.3 1.2 %copy-start = (bf16[1,4096,128]{2,1,0:T(8,128)(2,1)S(1)}, bf16[1,4096,128]{2,1,0:T(8,128)(2,1)}, u32[]{:S(2)}) copy-start(bf16[1,4096,128]{2,1,0:T(8,128)(2,1)} %param.5) | copy-start | bytes 3145732
  2.5 1.2 %copy-start.1 = (bf16[1,4096,128]{2,1,0:T(8,128)(2,1)S(1)}, bf16[1,4096,128]{2,1,0:T(8,128)(2,1)}, u32[]{:S(2)}) copy-start(bf16[1,4096,128]{2,1,0:T(8,128)(2,1)} %param.6) | copy-start | bytes 3145732
  3.7 0.9 %copy-start.2 = (bf16[1,8,128,128]{3,2,1,0:T(8,128)(2,1)S(1)}, bf16[1,8,128,128]{3,2,1,0:T(8,128)(2,1)}, u32[]{:S(2)}) copy-start(bf16[1,8,128,128]{3,2,1,0:T(8,128)(2,1)} %param.4) | copy-start | bytes 786436
where the time goes:
time: 34 us; the launch traced here: 33.7 us
  Pallas kernels  27.2 us (80%)
  local copies, waits for them, and re-layouts  5.88 us (17%)
  between operations  0.65 us (2%)
    pallas_call x1, Pallas kernels, shards(): pl.pallas_call(functools.partial(kernel, cfg), out_shape=(jax.ShapeDtypeS...  27.2 us
    unnamed x11, local copies, waits for them, and re-layouts  5.88 us

commit v1 on v0

--- a/solution.py
+++ b/solution.py
@@ -385,7 +385,24 @@
             compiler_params=pltpu.CompilerParams(
                 collective_id=0, has_side_effects=True, vmem_limit_bytes=50 * 1024 * 1024
             ),
-        )(queries[0].reshape(rows, width), cache_keys[0], cache_values[0], sel_index)
+        )(*[pltpu.with_memory_space_constraint(a, pltpu.HBM) for a in (queries[0].reshape(rows, width), cache_keys[0], cache_values[0], sel_index)])
+        def emit(a_ref, b_ref, c_ref, d_ref, e_ref, f_ref, sems):
+            copies = [
+                pltpu.make_async_copy(src, dst, sems.at[i])
+                for i, (src, dst) in enumerate(((a_ref, d_ref), (b_ref, e_ref), (c_ref, f_ref)))
+            ]
+            for c in copies:
+                c.start()
+            for c in copies:
+                c.wait()
+
+        gram, rhs, gap = pl.pallas_call(
+            emit,
+            out_shape=tuple(jax.ShapeDtypeStruct(a.shape, f32) for a in (gram, rhs, gap)),
+            in_specs=[pl.BlockSpec(memory_space=pltpu.VMEM)] * 3,
+            out_specs=(pl.BlockSpec(memory_space=pltpu.HBM),) * 3,
+            scratch_shapes=[dma((3,))],
+        )(*[pltpu.with_memory_space_constraint(a, pltpu.VMEM) for a in (gram, rhs, gap)])
         return gram[None], rhs[None], gap.reshape(1, heads, rows_dev)
 
     in_specs = (

time: 34 us -> 28.6 us (0.84)
  local copies, waits for them, and re-layouts: 5.88 us -> 0 us
  Pallas kernels: 27.2 us -> 27.8 us
    unnamed x11 -> x0, local copies, waits for them, and re-layouts: 5.88 us -> none
    pallas_call x0 -> x1, Pallas kernels: none -> 0.66 us  [shards(): pl.pallas_call(emit, out_shape=tuple((jax.ShapeDtypeStruct(a.shape, f32)...]
where the time goes in v1:
time: 28.6 us; the launch traced here: 28.5 us
  Pallas kernels  27.8 us (97%)
  between operations  0.64 us (2%)
    pallas_call x1, Pallas kernels, shards(): pl.pallas_call(functools.partial(kernel, cfg), out_shape=(jax.ShapeDtypeS...  27.2 us
    pallas_call x1, Pallas kernels, shards(): pl.pallas_call(emit, out_shape=tuple((jax.ShapeDtypeStruct(a.shape, f32)...  0.66 us

profile of v1, /device:TPU:1, one launch (start us, length us, event | category | flops | bytes accessed | tf_op | source)
XLA Modules:
  0.0 28.5 jit_solution(9517339879756381351)
XLA Ops:
  0.6 27.2 %shard_map.67 = (f32[32,512]{1,0:T(8,128)S(1)}, f32[32,128]{1,0:T(8,128)S(1)}, f32[8,128]{1,0:T(8,128)S(1)}) custom-call(bf16[1024,128]{1,0:T(8,128)(2,1)} %bitcast.8, bf16[4096,128]{1,0:T(8,128)(2,1)} %bitcast.6, bf16[4096,128]{1,0:T(8,128)(2,1)} %bitcast.7, s32[1,64]{1,0:T(1,128)} %sel_hbm.1), custom_call_target="tpu_custom_call" | custom-call | tf_op jit(solution)/shard_map/pallas_call | solution.py:353
  27.8 0.7 %shard_map.68 = (f32[32,512]{1,0:T(8,128)}, f32[32,128]{1,0:T(8,128)}, f32[8,128]{1,0:T(8,128)}) custom-call(f32[32,512]{1,0:T(8,128)S(1)} %get-tuple-element.9.a_ref, f32[32,128]{1,0:T(8,128)S(1)} %get-tuple-element.10.b_ref, f32[8,128]{1,0:T(8,128)S(1)} %get-tuple-element.11.c_ref), custom_call_target="tpu_custom_call" | custom-call | tf_op jit(solution)/shard_map/pallas_call | solution.py:399

commit v2 on v0

v2 whole, which is shorter than its diff:
```python
import functools
import math

import jax
import jax.numpy as jnp
from jax import lax
from jax.experimental import pallas as pl
from jax.experimental.pallas import tpu as pltpu
from jax.sharding import PartitionSpec as P

MESH = pl.DeviceIdType.MESH
eps = 1e-06
ln2 = math.log(2.0)
top16 = 32767.0
f32 = jnp.float32
bf16 = jnp.bfloat16
i16 = jnp.int16


def dot_nt(a, b):
    return lax.dot_general(a, b, (((1,), (1,)), ((), ())), preferred_element_type=f32)


def fold(x, op, height):
    rows, cols = x.shape
    return op(x.reshape(rows // height, height, cols), axis=0)


def encode(x):
    peak = jnp.maximum(jnp.max(jnp.abs(x), axis=0, keepdims=True), 1e-30)
    codes = jnp.floor(x * (top16 / peak) + 0.5)
    return codes.astype(jnp.int32).astype(i16), peak * (1.0 / top16)


def decode(codes, step):
    return codes.astype(jnp.int32).astype(f32) * step


def far_first(i, t, n):
    flip = i // (n // 2)
    low = i + flip * (n - 1 - 2 * i)
    other = n - 1 - t - (low + t) // (n - 1)
    return other + flip * (n - 1 - 2 * other)


def kernel(
    cfg, q_hbm, k_hbm, v_hbm, sel_hbm, gram_ref, rhs_ref, gap_ref,
    q_ref, k_ref, v_ref, sel_ref, vt, sa, sb, acc, comp,
    both, code, cstat, xcode, xstat, zcode, zstat, zrcode, zrstat,
    feat, mass, gpart, grecv, fsend, frecv, ysend, yrecv, rcode, rstat, rrcode, rrstat, in_sem,
    csend_sem, crecv_sem, xsend_sem, xrecv_sem, zsend_sem, zrecv_sem, gsend_sem, grecv_sem,
    fsend_sem, frecv_sem, ysend_sem, yrecv_sem, rsend_sem, rrecv_sem,
):
    loads = [
        pltpu.make_async_copy(src, dst, in_sem.at[i])
        for i, (src, dst) in enumerate(
            ((sel_hbm, sel_ref), (k_hbm, k_ref), (q_hbm, q_ref), (v_hbm, v_ref))
        )
    ]
    for load in loads:
        load.start()
    n, npb = cfg["n"], cfg["npb"]
    rows, width = q_ref.shape
    keys = k_ref.shape[0]
    sel_dev = sel_ref.shape[1]
    sel_all = n * sel_dev
    piece = sel_dev // npb
    chunk = rows // n
    per = cfg["per"]
    block = per * chunk
    groups = n // per
    scale = width ** (-0.5)
    c2 = scale * math.log2(math.e)
    first_tile, tile, height = cfg["first_tile"], cfg["tile"], 32
    inverse = 1.0 / (rows * npb)

    me = lax.axis_index("ctx")
    pb = lax.axis_index("pb")
    my_group = me // per
    my_pair = me // 2
    side = lax.rem(me, 2)

    barrier = pltpu.get_barrier_semaphore()

    def greet(j, carry):
        for d in range(npb):
            @pl.when(jnp.logical_or(j > 0, d > 0))
            def _():
                pl.semaphore_signal(
                    barrier, inc=1,
                    device_id={"ctx": lax.rem(me + j, n), "pb": lax.rem(pb + d, npb)},
                    device_id_type=MESH,
                )
        return carry

    lax.fori_loop(0, n, greet, 0)

    def comp_copy(j, src):
        return pltpu.make_async_remote_copy(
            src_ref=comp.at[src], dst_ref=comp.at[src],
            send_sem=csend_sem.at[j], recv_sem=crecv_sem.at[src],
            device_id={"ctx": j}, device_id_type=MESH,
        )

    def x_copies(a):
        there = {"ctx": me + 1 - 2 * side}
        return [
            pltpu.make_async_remote_copy(
                src_ref=src.at[a, 1 - side], dst_ref=dst.at[a],
                send_sem=xsend_sem.at[i, a], recv_sem=xrecv_sem.at[i, a],
                device_id=there, device_id_type=MESH,
            )
            for i, (src, dst) in enumerate(((code, xcode), (cstat, xstat)))
        ]

    def z_copies(a, src_pair):
        there = {"ctx": 2 * a + side}
        return [
            pltpu.make_async_remote_copy(
                src_ref=src.at[a], dst_ref=dst.at[src_pair],
                send_sem=zsend_sem.at[i, a], recv_sem=zrecv_sem.at[i, src_pair],
                device_id=there, device_id_type=MESH,
            )
            for i, (src, dst) in enumerate(((zcode, zrcode), (zstat, zrstat)))
        ]

    def pb_copy(send, recv, send_sem, recv_sem, d, src):
        return pltpu.make_async_remote_copy(
            src_ref=send.at[d], dst_ref=recv.at[src],
            send_sem=send_sem.at[d], recv_sem=recv_sem.at[src],
            device_id={"pb": d}, device_id_type=MESH,
        )

    def g_copy(d, src):
        return pb_copy(gpart, grecv, gsend_sem, grecv_sem, d, src)

    def f_copy(d, src):
        return pb_copy(fsend, frecv, fsend_sem, frecv_sem, d, src)

    def y_copy(d, src):
        return pltpu.make_async_remote_copy(
            src_ref=ysend, dst_ref=yrecv.at[src],
            send_sem=ysend_sem.at[d], recv_sem=yrecv_sem.at[src],
            device_id={"pb": d}, device_id_type=MESH,
        )

    def r_copies(j, src_ctx):
        return [
            pltpu.make_async_remote_copy(
                src_ref=src.at[j], dst_ref=dst.at[src_ctx],
                send_sem=rsend_sem.at[i, j], recv_sem=rrecv_sem.at[i, src_ctx],
                device_id={"ctx": j}, device_id_type=MESH,
            )
            for i, (src, dst) in enumerate(((rcode, rrcode), (rstat, rrstat)))
        ]

    def stats(top, total, step):
        return jnp.concatenate([top, total, step, jnp.zeros((5, top.shape[1]), f32)], axis=0)

    def merge(parts):
        top = parts[0][1][0:1, :]
        for _, stat in parts[1:]:
            top = jnp.maximum(top, stat[0:1, :])
        total, summed = 0.0, 0.0
        for part, stat in parts:
            weight = jnp.exp2(stat[0:1, :] - top)
            total += weight * stat[1:2, :]
            summed += weight * part()
        return top, total, summed

    def pass_on(t):
        first = group_of(t) * (per // 2)
        for u in range(per // 2):
            a = first + u
            for copy in x_copies(a):
                copy.wait_recv()
            theirs, ours = xstat[a], cstat[a, side]
            top, total, summed = merge([
                (lambda: both[a, side], ours),
                (lambda: decode(xcode[a], theirs[2:3, :]), theirs),
            ])
            codes, step = encode(summed)
            line = stats(top, total, step)
            if t == groups - 1:
                @pl.when(a == my_pair)
                def _():
                    zrcode[my_pair] = codes
                    zrstat[my_pair] = line

                @pl.when(a != my_pair)
                def _():
                    zcode[a] = codes
                    zstat[a] = line
                    for copy in z_copies(a, my_pair):
                        copy.start()
            else:
                zcode[a] = codes
                zstat[a] = line
                for copy in z_copies(a, my_pair):
                    copy.start()

    def group_of(t):
        return my_group if t == groups - 1 else far_first(my_group, t, groups)

    def load_q(t):
        q = q_ref[pl.ds(pl.multiple_of(group_of(t) * block, block), block), :].astype(f32) * c2
        high = q.astype(bf16)
        return jnp.concatenate([high, (q - high.astype(f32)).astype(bf16)], axis=1)

    def at(i, size):
        return pl.ds(pl.multiple_of(i * size, size), size)

    def score_tile(buf, q, where, top):
        k = k_ref[where, :]
        s = dot_nt(jnp.concatenate([k, k], axis=1), q)
        buf[where, :] = s
        return jnp.maximum(top, fold(s, jnp.max, height))

    def send_comp(t, carry):
        comp_copy(far_first(me, t, n), me).start()
        return carry

    lowest = jnp.full((height, block), -jnp.inf, f32)
    with jax.named_scope("w_k"):
        for load in loads[:3]:
            load.wait()
    pos = (sel_ref[...] - me * keys).astype(f32)
    diag = lax.broadcasted_iota(jnp.int32, (sel_dev, sel_dev), 0) == lax.broadcasted_iota(
        jnp.int32, (sel_dev, sel_dev), 1
    )
    column = jnp.sum(jnp.where(diag, pos, 0.0), axis=1, keepdims=True).astype(jnp.int32)
    q = load_q(0)

    def first_scores(i, carry):
        top, picked = carry
        where = at(i, first_tile)
        top = score_tile(sa, q, where, top)
        hot = lax.broadcasted_iota(jnp.int32, (sel_dev, first_tile), 1) == column - i * first_tile
        picked += jnp.dot(hot.astype(f32).astype(bf16), k_ref[where, :], preferred_element_type=f32)
        return top, picked

    top, picked = lax.fori_loop(
        0, keys // first_tile, first_scores, (lowest, jnp.zeros((sel_dev, width), f32))
    )
    comp[me] = picked.astype(bf16)
    with jax.named_scope("w_v"):
        loads[3].wait()

    for t in range(groups):
        row_max = jnp.max(top, axis=0, keepdims=True)
        shift = jnp.broadcast_to(row_max, (8, block))
        now, later = (sa, sb) if t % 2 == 0 else (sb, sa)
        q = load_q(t + 1) if t + 1 < groups else None
        acc[...] = jnp.zeros((width, block), f32)

        def body(i, carry, t=t, q=q, shift=shift, now=now, later=later):
            top, total = carry
            where = at(i, tile)
            x = now[where, :].reshape(tile // 8, 8, block) - shift[None]
            p = jnp.exp2(x).reshape(tile, block)
            total += fold(p, jnp.sum, height)
            if t == 0:
                v = v_ref[where, :].T
                vt[:, where] = v
            else:
                v = vt[:, where]
            acc[...] += jnp.dot(v, p.astype(bf16), preferred_element_type=f32)
            if t + 1 < groups:
                top = score_tile(later, q, where, top)
            return top, total

        top, total = lax.fori_loop(
            0, keys // tile, body, (lowest, jnp.zeros((height, block), f32))
        )
        row_total = jnp.sum(total, axis=0, keepdims=True)
        first = group_of(t) * (per // 2)
        for u in range(per // 2):
            for e in range(2):
                lanes = slice((2 * u + e) * chunk, (2 * u + e + 1) * chunk)
                part = acc[:, lanes]
                codes, step = encode(part)
                both[first + u, e] = part
                code[first + u, e] = codes
                cstat[first + u, e] = stats(row_max[:, lanes], row_total[:, lanes], step)
        if t == 0:
            with jax.named_scope("w_bar"):
                pl.semaphore_wait(barrier, n * npb - 1)
        for u in range(per // 2):
            for copy in x_copies(first + u):
                copy.start()
        if t == 0:
            lax.fori_loop(0, n - 1, send_comp, 0)
        if t > 1:
            with jax.named_scope("pass%d" % (t - 2)):
                pass_on(t - 2)

    def wait_comp(d, carry):
        src = lax.rem(me + d, n)
        comp_copy(src, src).wait_recv()
        return carry

    with jax.named_scope("w_comp"):
        lax.fori_loop(1, n, wait_comp, 0)

    def features(g):
        compact = comp[...].reshape(sel_all, width)
        c = dot_nt(compact, q_ref[g * block : (g + 1) * block, :])
        cmax = jnp.max(c, axis=0, keepdims=True)
        e = jnp.exp2(c * c2 - cmax * c2)
        ctotal = jnp.sum(e, axis=0, keepdims=True)
        f = (e * (sel_all / ctotal)).astype(bf16)
        line = jnp.broadcast_to(cmax * scale + jnp.log(ctotal), (8, block))
        for u in range(per):
            feat[g * per + u] = f[:, u * chunk : (u + 1) * chunk]
            mass[g * per + u] = line[:, u * chunk : (u + 1) * chunk]

    with jax.named_scope("features"):
        for g in range(groups):
            features(g)
    if groups > 1:
        with jax.named_scope("pass%d" % (groups - 2)):
            pass_on(groups - 2)

    for d in range(npb):
        for j in range(n):
            start = (j * npb + d) * piece
            fsend[d, j * piece : (j + 1) * piece, :] = feat[me, start : start + piece, :]
    for d in range(1, npb):
        f_copy(lax.rem(pb + d, npb), pb).start()

    with jax.named_scope("gram"):
        gram = jnp.zeros((sel_dev, sel_all), f32)
        own = pl.ds(pl.multiple_of(me * sel_dev, sel_dev), sel_dev)
        for c in range(n):
            gram += dot_nt(feat[c, own, :], feat[c])
    for d in range(npb):
        gpart[d] = gram[d * piece : (d + 1) * piece, :] * inverse
    for d in range(1, npb):
        g_copy(lax.rem(pb + d, npb), pb).start()

    with jax.named_scope("pass%d" % (groups - 1)):
        pass_on(groups - 1)

    def wait_z(d, carry):
        src = lax.rem(my_pair + d, n // 2)
        for copy in z_copies(src, src):
            copy.wait_recv()
        return carry

    with jax.named_scope("w_z"):
        lax.fori_loop(1, n // 2, wait_z, 0)
    lines = [zrstat[b] for b in range(n // 2)]
    top, total, summed = merge([
        (lambda b=b: decode(zrcode[b], lines[b][2:3, :]), lines[b]) for b in range(n // 2)
    ])
    target = summed / total
    y = (target * lax.rsqrt(jnp.mean(target * target, axis=0, keepdims=True) + eps)).astype(bf16)
    ysend[...] = y
    for d in range(1, npb):
        y_copy(lax.rem(pb + d, npb), pb).start()
    gap = top * ln2 + jnp.log(total) - mass[me, 0:1, :]
    rhs = dot_nt(fsend[pb], y)
    for d in range(1, npb):
        src = lax.rem(pb + d, npb)
        with jax.named_scope("w_y"):
            f_copy(pb, src).wait_recv()
            y_copy(pb, src).wait_recv()
        rhs += dot_nt(frecv[src], yrecv[src])
    rhs = rhs * inverse
    for j in range(n):
        codes, step = encode(rhs[j * piece : (j + 1) * piece, :])
        rcode[j] = codes
        rstat[j, 0:1, :width] = step
        rstat[j, 1:2, :chunk] = gap

    def send_r(t, carry):
        for copy in r_copies(far_first(me, t, n), me):
            copy.start()
        return carry

    lax.fori_loop(0, n - 1, send_r, 0)
    rrcode[me] = rcode[me]
    rrstat[me] = rstat[me]

    with jax.named_scope("w_g"):
        for d in range(1, npb):
            g_copy(pb, lax.rem(pb + d, npb)).wait_recv()
    result = gpart[pb]
    for d in range(1, npb):
        result += grecv[lax.rem(pb + d, npb)]
    gram_ref[...] = result

    for d in range(1, npb):
        there = lax.rem(pb + d, npb)
        for copy in (g_copy, f_copy, y_copy):
            copy(there, pb).wait_send()

    def drain(d, carry):
        comp_copy(lax.rem(me + d, n), me).wait_send()
        return carry

    lax.fori_loop(1, n, drain, 0)

    def drain_x(a, carry):
        for copy in x_copies(a):
            copy.wait_send()
        return carry

    lax.fori_loop(0, n // 2, drain_x, 0)

    def drain_z(d, carry):
        for copy in z_copies(lax.rem(my_pair + d, n // 2), my_pair):
            copy.wait_send()
        return carry

    lax.fori_loop(1, n // 2, drain_z, 0)

    def wait_r(d, carry):
        src = lax.rem(me + d, n)
        for copy in r_copies(src, src):
            copy.wait_recv()
        return carry

    with jax.named_scope("w_r"):
        lax.fori_loop(1, n, wait_r, 0)
    out = jnp.zeros((piece, width), f32)
    for j in range(n):
        out += decode(rrcode[j], rrstat[j, 0:1, :width])
        gap_ref[j : j + 1, :] = rrstat[j, 1:2, :chunk]
    rhs_ref[...] = out

    def drain_r(d, carry):
        for copy in r_copies(lax.rem(me + d, n), me):
            copy.wait_send()
        return carry

    lax.fori_loop(1, n, drain_r, 0)


def emit(*refs):
    count = (len(refs) - 1) // 2
    copies = [pltpu.make_async_copy(refs[i], refs[count + i], refs[-1].at[i]) for i in range(count)]
    for copy in copies:
        copy.start()
    for copy in copies:
        copy.wait()


def solution(mesh):
    n, npb = mesh.shape["ctx"], mesh.shape["pb"]

    def shards(queries, cache_keys, cache_values, sel_index):
        heads, rows_dev, width = queries.shape[1:]
        rows = heads * rows_dev
        keys = cache_keys.shape[1]
        sel_dev = sel_index.shape[1]
        sel_all, piece, chunk = sel_dev * n, sel_dev // npb, rows // n
        per = max(2, min(n, 256 // chunk))
        while n % per or per % 2:
            per -= 1
        block = per * chunk
        cfg = dict(n=n, npb=npb, per=per, first_tile=math.gcd(keys, 1024), tile=math.gcd(keys, 2048))
        lanes = max(width, chunk)
        pairs = n // 2
        vmem = pl.BlockSpec(memory_space=pltpu.VMEM)
        hbm = pl.BlockSpec(memory_space=pltpu.HBM)
        dma = pltpu.SemaphoreType.DMA
        results = (
            jax.ShapeDtypeStruct((piece, sel_all), f32),
            jax.ShapeDtypeStruct((piece, width), f32),
            jax.ShapeDtypeStruct((n, chunk), f32),
        )
        operands = (queries[0].reshape(rows, width), cache_keys[0], cache_values[0], sel_index)
        parts = pl.pallas_call(
            functools.partial(kernel, cfg),
            out_shape=results,
            in_specs=[hbm] * 4,
            out_specs=(vmem,) * 3,
            scratch_shapes=[
                pltpu.VMEM((rows, width), bf16),
                pltpu.VMEM((keys, width), bf16),
                pltpu.VMEM((keys, width), bf16),
                pltpu.VMEM((1, sel_dev), jnp.int32),
                pltpu.VMEM((width, keys), bf16),
                pltpu.VMEM((keys, block), f32),
                pltpu.VMEM((keys, block), f32),
                pltpu.VMEM((width, block), f32),
                pltpu.VMEM((n, sel_dev, width), bf16),
                pltpu.VMEM((pairs, 2, width, chunk), f32),
                pltpu.VMEM((pairs, 2, width, chunk), i16),
                pltpu.VMEM((pairs, 2, 8, chunk), f32),
                pltpu.VMEM((pairs, width, chunk), i16),
                pltpu.VMEM((pairs, 8, chunk), f32),
                pltpu.VMEM((pairs, width, chunk), i16),
                pltpu.VMEM((pairs, 8, chunk), f32),
                pltpu.VMEM((pairs, width, chunk), i16),
                pltpu.VMEM((pairs, 8, chunk), f32),
                pltpu.VMEM((n, sel_all, chunk), bf16),
                pltpu.VMEM((n, 8, chunk), f32),
                pltpu.VMEM((npb, piece, sel_all), f32),
                pltpu.VMEM((npb, piece, sel_all), f32),
                pltpu.VMEM((npb, n * piece, chunk), bf16),
                pltpu.VMEM((npb, n * piece, chunk), bf16),
                pltpu.VMEM((width, chunk), bf16),
                pltpu.VMEM((npb, width, chunk), bf16),
                pltpu.VMEM((n, piece, width), i16),
                pltpu.VMEM((n, 2, lanes), f32),
                pltpu.VMEM((n, piece, width), i16),
                pltpu.VMEM((n, 2, lanes), f32),
                dma((4,)),
                dma((n,)), dma((n,)), dma((2, pairs)), dma((2, pairs)), dma((2, pairs)), dma((2, pairs)),
                dma((npb,)), dma((npb,)), dma((npb,)), dma((npb,)), dma((npb,)), dma((npb,)),
                dma((2, n)), dma((2, n)),
            ],
            compiler_params=pltpu.CompilerParams(
                collective_id=0, has_side_effects=True, vmem_limit_bytes=50 * 1024 * 1024
            ),
        )(*[pltpu.with_memory_space_constraint(a, pltpu.HBM) for a in operands])
        gram, rhs, gap = pl.pallas_call(
            emit,
            out_shape=results,
            in_specs=[vmem] * 3,
            out_specs=(hbm,) * 3,
            scratch_shapes=[dma((3,))],
        )(*[pltpu.with_memory_space_constraint(a, pltpu.VMEM) for a in parts])
        return gram[None], rhs[None], gap.reshape(1, heads, rows_dev)

    in_specs = (
        P("kv", None, "pb", None),
        P("kv", "ctx", None),
        P("kv", "ctx", None),
        P("kv", "ctx"),
    )
    out_specs = (P("kv", ("ctx", "pb"), None), P("kv", ("ctx", "pb"), None), P("kv", None, "pb"))
    return jax.shard_map(shards, mesh=mesh, in_specs=in_specs, out_specs=out_specs, check_vma=False)
```

time: 34 us -> 23.3 us (0.69)
  local copies, waits for them, and re-layouts: 5.88 us -> 0 us
  Pallas kernels: 27.2 us -> 22.5 us
    unnamed x11 -> x0, local copies, waits for them, and re-layouts: 5.88 us -> none
    pallas_call x1 -> x2, Pallas kernels: 27.2 us -> 22.5 us  [the longest x1 21.9 us: shards(): pl.pallas_call(functools.partial(kernel, cfg), out_shape=results, in_spec...]
where the time goes in v2:
time: 23.3 us; the launch traced here: 23.2 us
  Pallas kernels  22.5 us (97%)
  between operations  0.64 us (3%)
    pallas_call x1, Pallas kernels, shards(): pl.pallas_call(functools.partial(kernel, cfg), out_shape=results, in_spec...  21.9 us
    pallas_call x1, Pallas kernels, shards(): pl.pallas_call(emit, out_shape=results, in_specs=[vmem] * 3, out_specs=(h...  0.66 us

profile of v2, /device:TPU:1, one launch (start us, length us, event | category | flops | bytes accessed | tf_op | source)
XLA Modules:
  0.0 23.2 jit_solution(2808223992645296528)
XLA Ops:
  0.6 21.9 %shard_map.67 = (f32[32,512]{1,0:T(8,128)S(1)}, f32[32,128]{1,0:T(8,128)S(1)}, f32[8,128]{1,0:T(8,128)S(1)}) custom-call(bf16[1024,128]{1,0:T(8,128)(2,1)} %bitcast.8, bf16[4096,128]{1,0:T(8,128)(2,1)} %bitcast.6, bf16[4096,128]{1,0:T(8,128)(2,1)} %bitcast.7, s32[1,64]{1,0:T(1,128)} %sel_hbm.1), custom_call_target="tpu_custom_call" | custom-call | tf_op jit(solution)/shard_map/pallas_call | solution.py:474
  22.5 0.7 %shard_map.68 = (f32[32,512]{1,0:T(8,128)}, f32[32,128]{1,0:T(8,128)}, f32[8,128]{1,0:T(8,128)}) custom-call(f32[32,512]{1,0:T(8,128)S(1)} %get-tuple-element.9.refs_0_, f32[32,128]{1,0:T(8,128)S(1)} %get-tuple-element.10.refs_1_, f32[8,128]{1,0:T(8,128)S(1)} %get-tuple-element.11.refs_2_), custom_call_target="tpu_custom_call" | custom-call | tf_op jit(solution)/shard_map/pallas_call | solution.py:519

commit v3 on v2

--- a/solution.py
+++ b/solution.py
@@ -48,8 +48,8 @@
     q_ref, k_ref, v_ref, sel_ref, vt, sa, sb, acc, comp,
     both, code, cstat, xcode, xstat, zcode, zstat, zrcode, zrstat,
     feat, mass, gpart, grecv, fsend, frecv, ysend, yrecv, rcode, rstat, rrcode, rrstat, in_sem,
-    csend_sem, crecv_sem, xsend_sem, xrecv_sem, zsend_sem, zrecv_sem, gsend_sem, grecv_sem,
-    fsend_sem, frecv_sem, ysend_sem, yrecv_sem, rsend_sem, rrecv_sem,
+    csend_sem, crecv_sem, xsend_sem, xrecv_sem, zsend_sem, zrecv_sem,
+    gsend_sem, grecv_sem, fsend_sem, frecv_sem, ysend_sem, yrecv_sem, rsend_sem, rrecv_sem,
 ):
     loads = [
         pltpu.make_async_copy(src, dst, in_sem.at[i])
@@ -71,7 +71,7 @@
     groups = n // per
     scale = width ** (-0.5)
     c2 = scale * math.log2(math.e)
-    first_tile, tile, height = cfg["first_tile"], cfg["tile"], 32
+    tile, height = cfg["tile"], 32
     inverse = 1.0 / (rows * npb)
 
     me = lax.axis_index("ctx")
@@ -95,11 +95,18 @@
 
     lax.fori_loop(0, n, greet, 0)
 
-    def comp_copy(j, src):
+    def comp_copy(j):
         return pltpu.make_async_remote_copy(
-            src_ref=comp.at[src], dst_ref=comp.at[src],
-            send_sem=csend_sem.at[j], recv_sem=crecv_sem.at[src],
+            src_ref=comp.at[me], dst_ref=comp.at[me],
+            send_sem=csend_sem, recv_sem=crecv_sem,
             device_id={"ctx": j}, device_id_type=MESH,
+        )
+
+    def all_comp():
+        slots = comp.at[pl.ds(0, n - 1)]
+        return pltpu.make_async_remote_copy(
+            src_ref=slots, dst_ref=slots, send_sem=csend_sem, recv_sem=crecv_sem,
+            device_id={"ctx": me}, device_id_type=MESH,
         )
 
     def x_copies(a):
@@ -107,21 +114,57 @@
         return [
             pltpu.make_async_remote_copy(
                 src_ref=src.at[a, 1 - side], dst_ref=dst.at[a],
-                send_sem=xsend_sem.at[i, a], recv_sem=xrecv_sem.at[i, a],
+                send_sem=xsend_sem.at[i], recv_sem=xrecv_sem.at[i, a],
                 device_id=there, device_id_type=MESH,
             )
             for i, (src, dst) in enumerate(((code, xcode), (cstat, xstat)))
         ]
 
-    def z_copies(a, src_pair):
+    def z_copies(a):
         there = {"ctx": 2 * a + side}
         return [
             pltpu.make_async_remote_copy(
-                src_ref=src.at[a], dst_ref=dst.at[src_pair],
-                send_sem=zsend_sem.at[i, a], recv_sem=zrecv_sem.at[i, src_pair],
+                src_ref=src.at[a], dst_ref=dst.at[my_pair],
+                send_sem=zsend_sem.at[i], recv_sem=zrecv_sem.at[i],
                 device_id=there, device_id_type=MESH,
             )
             for i, (src, dst) in enumerate(((zcode, zrcode), (zstat, zrstat)))
+        ]
+
+    def r_copies(j):
+        return [
+            pltpu.make_async_remote_copy(
+                src_ref=src.at[j], dst_ref=dst.at[me],
+                send_sem=rsend_sem.at[i], recv_sem=rrecv_sem.at[i],
+                device_id={"ctx": j}, device_id_type=MESH,
+            )
+            for i, (src, dst) in enumerate(((rcode, rrcode), (rstat, rrstat)))
+        ]
+
+    def together(pairs, send_sem, recv_sem, count):
+        return [
+            pltpu.make_async_remote_copy(
+                src_ref=src.at[pl.ds(0, count)], dst_ref=dst.at[pl.ds(0, count)],
+                send_sem=send_sem.at[i], recv_sem=recv_sem.at[i],
+                device_id={"ctx": me}, device_id_type=MESH,
+            )
+            for i, (src, dst) in enumerate(pairs)
+        ]
+
+    def all_z():
+        return together(((zcode, zrcode), (zstat, zrstat)), zsend_sem, zrecv_sem, n // 2 - 1)
+
+    def all_r():
+        return together(((rcode, rrcode), (rstat, rrstat)), rsend_sem, rrecv_sem, n - 1)
+
+    def all_x():
+        return [
+            pltpu.make_async_remote_copy(
+                src_ref=src.at[:, 0], dst_ref=src.at[:, 0],
+                send_sem=xsend_sem.at[i], recv_sem=xrecv_sem.at[i, 0],
+                device_id={"ctx": me}, device_id_type=MESH,
+            )
+            for i, src in enumerate((code, cstat))
         ]
 
     def pb_copy(send, recv, send_sem, recv_sem, d, src):
@@ -143,16 +186,6 @@
             send_sem=ysend_sem.at[d], recv_sem=yrecv_sem.at[src],
             device_id={"pb": d}, device_id_type=MESH,
         )
-
-    def r_copies(j, src_ctx):
-        return [
-            pltpu.make_async_remote_copy(
-                src_ref=src.at[j], dst_ref=dst.at[src_ctx],
-                send_sem=rsend_sem.at[i, j], recv_sem=rrecv_sem.at[i, src_ctx],
-                device_id={"ctx": j}, device_id_type=MESH,
-            )
-            for i, (src, dst) in enumerate(((rcode, rrcode), (rstat, rrstat)))
-        ]
 
     def stats(top, total, step):
         return jnp.concatenate([top, total, step, jnp.zeros((5, top.shape[1]), f32)], axis=0)
@@ -191,12 +224,12 @@
                 def _():
                     zcode[a] = codes
                     zstat[a] = line
-                    for copy in z_copies(a, my_pair):
+                    for copy in z_copies(a):
                         copy.start()
             else:
                 zcode[a] = codes
                 zstat[a] = line
-                for copy in z_copies(a, my_pair):
+                for copy in z_copies(a):
                     copy.start()
 
     def group_of(t):
@@ -216,44 +249,31 @@
         buf[where, :] = s
         return jnp.maximum(top, fold(s, jnp.max, height))
 
-    def send_comp(t, carry):
-        comp_copy(far_first(me, t, n), me).start()
-        return carry
-
     lowest = jnp.full((height, block), -jnp.inf, f32)
-    with jax.named_scope("w_k"):
-        for load in loads[:3]:
-            load.wait()
-    pos = (sel_ref[...] - me * keys).astype(f32)
-    diag = lax.broadcasted_iota(jnp.int32, (sel_dev, sel_dev), 0) == lax.broadcasted_iota(
-        jnp.int32, (sel_dev, sel_dev), 1
-    )
-    column = jnp.sum(jnp.where(diag, pos, 0.0), axis=1, keepdims=True).astype(jnp.int32)
-    q = load_q(0)
-
-    def first_scores(i, carry):
-        top, picked = carry
-        where = at(i, first_tile)
-        top = score_tile(sa, q, where, top)
-        hot = lax.broadcasted_iota(jnp.int32, (sel_dev, first_tile), 1) == column - i * first_tile
-        picked += jnp.dot(hot.astype(f32).astype(bf16), k_ref[where, :], preferred_element_type=f32)
-        return top, picked
-
-    top, picked = lax.fori_loop(
-        0, keys // first_tile, first_scores, (lowest, jnp.zeros((sel_dev, width), f32))
-    )
-    comp[me] = picked.astype(bf16)
-    with jax.named_scope("w_v"):
-        loads[3].wait()
-
-    for t in range(groups):
-        row_max = jnp.max(top, axis=0, keepdims=True)
-        shift = jnp.broadcast_to(row_max, (8, block))
+
+    def first_scores():
+        q, column = load_q(0), column_of()
+
+        def body(i, carry):
+            top, picked = carry
+            where = at(i, tile)
+            top = score_tile(sa, q, where, top)
+            hot = lax.broadcasted_iota(jnp.int32, (sel_dev, tile), 1) == column - i * tile
+            picked += jnp.dot(hot.astype(f32).astype(bf16), k_ref[where, :], preferred_element_type=f32)
+            return top, picked
+
+        start = (lowest, jnp.zeros((sel_dev, width), f32))
+        top, picked = lax.fori_loop(0, keys // tile, body, start)
+        comp[me] = picked.astype(bf16)
+        return top
+
+    def attend(t, top):
+        shift = jnp.broadcast_to(jnp.max(top, axis=0, keepdims=True), (8, block))
         now, later = (sa, sb) if t % 2 == 0 else (sb, sa)
         q = load_q(t + 1) if t + 1 < groups else None
         acc[...] = jnp.zeros((width, block), f32)
 
-        def body(i, carry, t=t, q=q, shift=shift, now=now, later=later):
+        def body(i, carry):
             top, total = carry
             where = at(i, tile)
             x = now[where, :].reshape(tile // 8, 8, block) - shift[None]
@@ -272,35 +292,70 @@
         top, total = lax.fori_loop(
             0, keys // tile, body, (lowest, jnp.zeros((height, block), f32))
         )
-        row_total = jnp.sum(total, axis=0, keepdims=True)
+        return top, jnp.sum(total, axis=0, keepdims=True), acc[...]
+
+    def send_comp(t, carry):
+        comp_copy(far_first(me, t, n)).start()
+        return carry
+
+    def column_of():
+        pos = (sel_ref[...] - me * keys).astype(f32)
+        diag = lax.broadcasted_iota(jnp.int32, (sel_dev, sel_dev), 0) == lax.broadcasted_iota(
+            jnp.int32, (sel_dev, sel_dev), 1
+        )
+        return jnp.sum(jnp.where(diag, pos, 0.0), axis=1, keepdims=True).astype(jnp.int32)
+
+    with jax.named_scope("w_k"):
+        for load in loads[:3]:
+            load.wait()
+    late = my_group == groups - 1
+
+    def open_sends():
+        pl.semaphore_wait(barrier, n * npb - 1)
+
+    def start_comp():
+        lax.fori_loop(0, n - 1, send_comp, 0)
+
+    top = first_scores()
+
+    @pl.when(late)
+    def _():
+        with jax.named_scope("w_bar_late"):
+            open_sends()
+        start_comp()
+
+    with jax.named_scope("w_v"):
+        loads[3].wait()
+
+    for t in range(groups):
+        row_max = jnp.max(top, axis=0, keepdims=True)
+        top, row_total, summed = attend(t, top)
         first = group_of(t) * (per // 2)
         for u in range(per // 2):
             for e in range(2):
                 lanes = slice((2 * u + e) * chunk, (2 * u + e + 1) * chunk)
-                part = acc[:, lanes]
+                part = summed[:, lanes]
                 codes, step = encode(part)
                 both[first + u, e] = part
                 code[first + u, e] = codes
                 cstat[first + u, e] = stats(row_max[:, lanes], row_total[:, lanes], step)
         if t == 0:
-            with jax.named_scope("w_bar"):
-                pl.semaphore_wait(barrier, n * npb - 1)
+            @pl.when(jnp.logical_not(late))
+            def _():
+                with jax.named_scope("w_bar"):
+                    open_sends()
+
         for u in range(per // 2):
             for copy in x_copies(first + u):
                 copy.start()
         if t == 0:
-            lax.fori_loop(0, n - 1, send_comp, 0)
-        if t > 1:
-            with jax.named_scope("pass%d" % (t - 2)):
-                pass_on(t - 2)
-
-    def wait_comp(d, carry):
-        src = lax.rem(me + d, n)
-        comp_copy(src, src).wait_recv()
-        return carry
-
+            pl.when(jnp.logical_not(late))(start_comp)
+
+    for t in range(groups - 2):
+        with jax.named_scope("pass%d" % t):
+            pass_on(t)
     with jax.named_scope("w_comp"):
-        lax.fori_loop(1, n, wait_comp, 0)
+        all_comp().wait_recv()
 
     def features(g):
         compact = comp[...].reshape(sel_all, width)
@@ -341,14 +396,9 @@
     with jax.named_scope("pass%d" % (groups - 1)):
         pass_on(groups - 1)
 
-    def wait_z(d, carry):
-        src = lax.rem(my_pair + d, n // 2)
-        for copy in z_copies(src, src):
+    with jax.named_scope("w_z"):
+        for copy in all_z():
             copy.wait_recv()
-        return carry
-
-    with jax.named_scope("w_z"):
-        lax.fori_loop(1, n // 2, wait_z, 0)
     lines = [zrstat[b] for b in range(n // 2)]
     top, total, summed = merge([
         (lambda b=b: decode(zrcode[b], lines[b][2:3, :]), lines[b]) for b in range(n // 2)
@@ -374,7 +424,7 @@
         rstat[j, 1:2, :chunk] = gap
 
     def send_r(t, carry):
-        for copy in r_copies(far_first(me, t, n), me):
+        for copy in r_copies(far_first(me, t, n)):
             copy.start()
         return carry
 
@@ -394,47 +444,21 @@
         there = lax.rem(pb + d, npb)
         for copy in (g_copy, f_copy, y_copy):
             copy(there, pb).wait_send()
-
-    def drain(d, carry):
-        comp_copy(lax.rem(me + d, n), me).wait_send()
-        return carry
-
-    lax.fori_loop(1, n, drain, 0)
-
-    def drain_x(a, carry):
-        for copy in x_copies(a):
-            copy.wait_send()
-        return carry
-
-    lax.fori_loop(0, n // 2, drain_x, 0)
-
-    def drain_z(d, carry):
-        for copy in z_copies(lax.rem(my_pair + d, n // 2), my_pair):
-            copy.wait_send()
-        return carry
-
-    lax.fori_loop(1, n // 2, drain_z, 0)
-
-    def wait_r(d, carry):
-        src = lax.rem(me + d, n)
-        for copy in r_copies(src, src):
+    all_comp().wait_send()
+    for copy in all_x() + all_z():
+        copy.wait_send()
+
+    with jax.named_scope("w_r"):
+        for copy in all_r():
             copy.wait_recv()
-        return carry
-
-    with jax.named_scope("w_r"):
-        lax.fori_loop(1, n, wait_r, 0)
     out = jnp.zeros((piece, width), f32)
     for j in range(n):
         out += decode(rrcode[j], rrstat[j, 0:1, :width])
         gap_ref[j : j + 1, :] = rrstat[j, 1:2, :chunk]
     rhs_ref[...] = out
 
-    def drain_r(d, carry):
-        for copy in r_copies(lax.rem(me + d, n), me):
-            copy.wait_send()
-        return carry
-
-    lax.fori_loop(1, n, drain_r, 0)
+    for copy in all_r():
+        copy.wait_send()
 
 
 def emit(*refs):
@@ -459,7 +483,7 @@
         while n % per or per % 2:
             per -= 1
         block = per * chunk
-        cfg = dict(n=n, npb=npb, per=per, first_tile=math.gcd(keys, 1024), tile=math.gcd(keys, 2048))
+        cfg = dict(n=n, npb=npb, per=per, tile=math.gcd(keys, 2048))
         lanes = max(width, chunk)
         pairs = n // 2
         vmem = pl.BlockSpec(memory_space=pltpu.VMEM)
@@ -508,9 +532,9 @@
                 pltpu.VMEM((n, piece, width), i16),
                 pltpu.VMEM((n, 2, lanes), f32),
                 dma((4,)),
-                dma((n,)), dma((n,)), dma((2, pairs)), dma((2, pairs)), dma((2, pairs)), dma((2, pairs)),
+                dma, dma, dma((2,)), dma((2, pairs)), dma((2,)), dma((2,)),
                 dma((npb,)), dma((npb,)), dma((npb,)), dma((npb,)), dma((npb,)), dma((npb,)),
-                dma((2, n)), dma((2, n)),
+                dma((2,)), dma((2,)),
             ],
             compiler_params=pltpu.CompilerParams(
                 collective_id=0, has_side_effects=True, vmem_limit_bytes=50 * 1024 * 1024

time: 23.3 us -> 22.3 us (0.957)
  Pallas kernels: 22.5 us -> 21.4 us
    pallas_call x1, Pallas kernels: 21.9 us -> 20.7 us  [shards(): pl.pallas_call(functools.partial(kernel, cfg), out_shape=results, in_spec...]
where the time goes in v3:
time: 22.3 us; the launch traced here: 22 us
  Pallas kernels  21.4 us (96%)
  between operations  0.64 us (3%)
    pallas_call x1, Pallas kernels, shards(): pl.pallas_call(functools.partial(kernel, cfg), out_shape=results, in_spec...  20.7 us
    pallas_call x1, Pallas kernels, shards(): pl.pallas_call(emit, out_shape=results, in_specs=[vmem] * 3, out_specs=(h...  0.66 us

profile of v3, /device:TPU:1, one launch (start us, length us, event | category | flops | bytes accessed | tf_op | source)
XLA Modules:
  0.0 22.0 jit_solution(2769589023862931781)
XLA Ops:
  0.6 20.7 %shard_map.67 = (f32[32,512]{1,0:T(8,128)S(1)}, f32[32,128]{1,0:T(8,128)S(1)}, f32[8,128]{1,0:T(8,128)S(1)}) custom-call(bf16[1024,128]{1,0:T(8,128)(2,1)} %bitcast.8, bf16[4096,128]{1,0:T(8,128)(2,1)} %bitcast.6, bf16[4096,128]{1,0:T(8,128)(2,1)} %bitcast.7, s32[1,64]{1,0:T(1,128)} %sel_hbm.1), custom_call_target="tpu_custom_call" | custom-call | tf_op jit(solution)/shard_map/pallas_call | solution.py:498
  21.4 0.7 %shard_map.68 = (f32[32,512]{1,0:T(8,128)}, f32[32,128]{1,0:T(8,128)}, f32[8,128]{1,0:T(8,128)}) custom-call(f32[32,512]{1,0:T(8,128)S(1)} %get-tuple-element.9.refs_0_, f32[32,128]{1,0:T(8,128)S(1)} %get-tuple-element.10.refs_1_, f32[8,128]{1,0:T(8,128)S(1)} %get-tuple-element.11.refs_2_), custom_call_target="tpu_custom_call" | custom-call | tf_op jit(solution)/shard_map/pallas_call | solution.py:543
